TPU v7x, 8 devices: a whole 2x2x1 slice. The times are simulated.
8 devices in a mesh: dp: 1 (over z), ep: 2 (over y), tp: 4 (over x, core).
Axes of the slice: x: 2, y: 2, z: 1, core: 2. Of those that a mesh axis runs over, the one named last changes fastest.
Arguments:
- x_in: bfloat16 [512, 1024], P(('dp', 'ep'))
- expert_ids: int32 [512, 8], P(('dp', 'ep'))
- gate_vals: float32 [512, 8], P(('dp', 'ep'))
- w_gate: bfloat16 [128, 1024, 1536], P('ep', None, 'tp')
- w_up: bfloat16 [128, 1024, 1536], P('ep', None, 'tp')
- w_down: bfloat16 [128, 1536, 1024], P('ep', 'tp')
Outputs:
- output: bfloat16 [512, 1024], P(('dp', 'ep'))
All inputs are finite; a program needn't handle non-finite values.
Results may differ from a plain program's by a relative error of at most 0.0101859.
Values are sent between devices in bfloat16 or wider.
A program may use at most 1 GiB of HBM per device.

v0:
```python
import jax
import jax.numpy as jnp
from jax import lax
from jax.sharding import PartitionSpec as P

CAP_NUM = 5
CAP_DEN = 4


def local_routing(expert_ids, n_experts, capacity):
    tokens, n_top = expert_ids.shape
    flat_ids = expert_ids.reshape(tokens * n_top)
    onehot = (flat_ids[:, None] == jnp.arange(n_experts, dtype=jnp.int32)[None, :]).astype(jnp.int32)
    slots = jnp.sum((jnp.cumsum(onehot, axis=0) - onehot) * onehot, axis=1)
    flat_slot = jnp.where(slots < capacity, flat_ids * capacity + slots, n_experts * capacity)
    token_num = jnp.broadcast_to(jnp.arange(tokens, dtype=jnp.int32)[:, None], (tokens, n_top)).reshape(tokens * n_top)
    slot_owner = jnp.full((n_experts * capacity + 1,), tokens, jnp.int32).at[flat_slot].set(token_num)
    return slot_owner[: n_experts * capacity].reshape(n_experts, capacity), flat_slot.reshape(tokens, n_top)


def solution(mesh):
    n_ep = mesh.shape['ep']
    n_tp = mesh.shape['tp']
    row_spec = P(('dp', 'ep'), None)

    def device_body(x_loc, ids_loc, gates_loc, wg_loc, wu_loc, wd_loc):
        tokens, d_model = x_loc.shape
        n_top = ids_loc.shape[1]
        local_experts = wg_loc.shape[0]
        n_experts = local_experts * n_ep
        capacity = CAP_NUM * n_top * tokens // (CAP_DEN * n_experts)
        slot_share = capacity // n_tp
        slot_owner, flat_slot = local_routing(ids_loc, n_experts, capacity)
        my_owner = lax.dynamic_slice_in_dim(slot_owner, lax.axis_index('tp') * slot_share, slot_share, axis=1)
        outgoing = jnp.take(x_loc, my_owner, axis=0, mode='fill', fill_value=0)
        outgoing = outgoing.reshape(n_ep, local_experts, slot_share, d_model)
        arrived = lax.all_to_all(outgoing, 'ep', 0, 2, tiled=True).reshape(local_experts, n_ep * slot_share, d_model)
        gathered = lax.all_gather(arrived, 'tp', axis=1, tiled=True)
        h_gate = jnp.einsum('erd,edf->erf', gathered, wg_loc, preferred_element_type=jnp.float32)
        h_up = jnp.einsum('erd,edf->erf', gathered, wu_loc, preferred_element_type=jnp.float32)
        hidden = (jax.nn.silu(h_gate) * h_up).astype(jnp.bfloat16)
        part_out = jnp.einsum('erf,efd->erd', hidden, wd_loc, preferred_element_type=jnp.float32).astype(jnp.bfloat16)
        part_out = part_out.reshape(local_experts, n_tp, n_ep * slot_share, d_model)
        pieces = lax.all_to_all(part_out, 'tp', 1, 1, tiled=True)
        y_mine = jnp.sum(pieces, axis=1, dtype=jnp.float32).astype(jnp.bfloat16)
        returned = lax.all_to_all(y_mine.reshape(local_experts, n_ep, slot_share, d_model), 'ep', 1, 0, tiled=True)
        returned = returned.reshape(n_experts, slot_share, d_model)
        y_all = lax.all_gather(returned, 'tp', axis=1, tiled=True).reshape(n_experts * capacity, d_model)
        picked = jnp.take(y_all, flat_slot, axis=0, mode='fill', fill_value=0)
        return jnp.sum(picked * gates_loc[:, :, None], axis=1).astype(jnp.bfloat16)

    return jax.shard_map(device_body, mesh=mesh,
                         in_specs=(row_spec, row_spec, row_spec, P('ep', None, 'tp'), P('ep', None, 'tp'), P('ep', 'tp', None)),
                         out_specs=row_spec, check_vma=False)
```

profile of v0, /device:TPU:0, one launch (start us, length us, event | category | flops | bytes accessed | tf_op | source)
XLA Modules:
  0.0 332.1 jit_solution(62130828806213513)
XLA Ops:
  6.5 0.9 copy.34
  7.8 0.3 fusion.11
  8.2 0.3 copy.37
  8.8 0.6 fusion.10
  9.5 8.1 %scatter_custom_fusion = s32[2561]{0:T(1024)S(1)} fusion(s32[2048]{0:T(1024)S(1)} %bitcast.43, s32[2048]{0:T(1024)S(1)} %reshape.120, s32[]{:T(128)} %constant.30.clone.1), kind=kCustom, calls=%fused_computation.30 | custom fusion | bytes 10248 | tf_op jit(solution)/shard_map/scatter | solution.py:17
  18.0 2.8 gather_fusion
  20.9 1.6 gather.11
  22.5 1.9 broadcast_select_fusion
  24.4 0.9 copy.41
  25.2 21.5 %all_to_all.35 = bf16[2,64,5,1024]{3,1,2,0:T(8,128)(2,1)} all-to-all(bf16[2,64,5,1024]{3,1,2,0:T(8,128)(2,1)S(1)} %copy.41), channel_id=1, replica_groups=mesh['dp'=1,'ep'=2,'tp'=4] {'ep'}, dimensions={0} | all-to-all | bytes 2621440 | tf_op jit(solution)/shard_map/all_to_all | solution.py:37
  46.7 0.2 all-gather.5.cloned.1.call-start
  47.0 37.7 %all-gather.3.cloned.1.call-done = bf16[64,40,1024]{2,0,1:T(8,128)(2,1)} async-done(((bf16[64,10,1024]{2,0,1:T(8,128)(2,1)}), bf16[64,40,1024]{2,0,1:T(8,128)(2,1)}) %all-gather.3.cloned.1.call-update) | async-done | bytes 5242896 | tf_op jit(solution)/shard_map/all_gather | solution.py:38
  84.7 33.4 %fusion = f32[64,40,384]{2,1,0:T(8,128)} fusion(bf16[64,1024,384]{2,1,0:T(8,128)(2,1)} %param.10, bf16[64,40,1024]{2,0,1:T(8,128)(2,1)} %all-gather.3.cloned.1.call-done), kind=kOutput, calls=%fused_computation.4 | convolution fusion | flops 2013265920 | bytes 59506688 | tf_op jit(solution)/shard_map/erd,edf->erf/dot_general | solution.py:40
  118.0 40.4 %convolution_convert_fusion = bf16[64,40,1024]{2,1,0:T(8,128)(2,1)} fusion(bf16[64,384,1024]{2,1,0:T(8,128)(2,1)} %param.11, f32[64,40,384]{2,1,0:T(8,128)} %fusion, bf16[64,1024,384]{2,1,0:T(8,128)(2,1)} %param.9, bf16[64,40,1024]{2,0,1:T(8,128)(2,1)} %all-gather.3.cloned.1.call-done), kind=kOutput, calls=%fused_computation.10 | convolution fusion | flops 4035051520 | bytes 115081216 | tf_op jit(solution)/shard_map/erf,efd->erd/dot_general | solution.py:42
  158.5 5.4 %copy.44 = bf16[64,40,1024]{2,0,1:T(8,128)(2,1)S(1)} copy(bf16[64,40,1024]{2,1,0:T(8,128)(2,1)} %convolution_convert_fusion) | data formatting | bytes 10485760 | tf_op jit(solution)/shard_map/convert_element_type | solution.py:42
  163.9 62.8 %all_to_all.36 = bf16[64,4,10,1024]{3,0,2,1:T(8,128)(2,1)} all-to-all(bf16[64,4,10,1024]{3,0,2,1:T(8,128)(2,1)S(1)} %bitcast.35), channel_id=1, replica_groups=mesh['dp'=1,'ep'=2,'tp'=4] {'tp'}, dimensions={1} | all-to-all | bytes 10485760 | tf_op jit(solution)/shard_map/all_to_all | solution.py:44
  226.6 3.9 %reduce_sum.37 = bf16[64,10,1024]{2,0,1:T(8,128)(2,1)S(1)} reduce(bf16[64,4,10,1024]{3,0,2,1:T(8,128)(2,1)} %all_to_all.36, bf16[]{:T(256)} %constant.52.clone.1), dimensions={1}, to_apply=%region_4.5 | reduce | flops 1966080 | bytes 6553602 | tf_op jit(solution)/shard_map/reduce_sum | solution.py:45
  230.5 18.8 %all_to_all.37 = bf16[64,2,5,1024]{3,0,2,1:T(8,128)(2,1)S(1)} all-to-all(bf16[64,2,5,1024]{3,0,2,1:T(8,128)(2,1)S(1)} %bitcast.39), channel_id=1, replica_groups=mesh['dp'=1,'ep'=2,'tp'=4] {'ep'}, dimensions={1} | all-to-all | bytes 2621440 | tf_op jit(solution)/shard_map/all_to_all | solution.py:46
  249.3 1.2 copy.45
  251.0 36.7 %all-gather.5.cloned.1.call-done = bf16[128,20,1024]{2,0,1:T(8,128)(2,1)} async-done(((bf16[128,5,1024]{2,0,1:T(8,128)(2,1)}), bf16[128,20,1024]{2,0,1:T(8,128)(2,1)}) %all-gather.5.cloned.1.call-update) | async-done | bytes 5242896 | tf_op jit(solution)/shard_map/all_gather | solution.py:48
  287.7 8.2 %copy.46 = bf16[128,20,1024]{2,1,0:T(8,128)(2,1)} copy(bf16[128,20,1024]{2,0,1:T(8,128)(2,1)} %all-gather.5.cloned.1.call-done) | data formatting | bytes 10485760 | tf_op jit(solution)/shard_map/all_gather | solution.py:48
  295.9 9.0 %reshape.99 = bf16[2560,1024]{1,0:T(8,128)(2,1)} reshape(bf16[128,20,1024]{2,1,0:T(8,128)(2,1)} %copy.46) | data formatting | bytes 10485760 | tf_op jit(solution)/shard_map/reshape | solution.py:48
  304.8 14.2 %gather_fusion.1 = bf16[2048,1024]{1,0:T(8,128)(2,1)} fusion(bf16[2560,1024]{1,0:T(8,128)(2,1)} %reshape.99, s32[2048]{0:T(1024)S(1)} %broadcast_clamp_fusion), kind=kCustom, calls=%fused_computation.1 | custom fusion | bytes 8396800 | tf_op jit(solution)/shard_map/jit(_take)/gather | solution.py:49
  319.0 6.2 %multiply_reduce_fusion = bf16[256,1024]{1,0:T(8,128)(2,1)} fusion(bf16[2048,1024]{1,0:T(8,128)(2,1)} %gather_fusion.1, f32[256,8]{1,0:T(8,128)S(1)} %copy.47, pred[256,8]{1,0:T(8,128)(4,1)S(1)} %get-tuple-element.5), kind=kLoop, calls=%fused_computation.3 | loop fusion | flops 8126464 | bytes 4728832 | tf_op jit(solution)/shard_map/reduce_sum | solution.py:50
  (30 shorter events, 1.5 us)
Async XLA Ops:
  6.5 11.5 %copy-start = (bf16[256,1024]{1,0:T(8,128)(2,1)S(1)}, bf16[256,1024]{1,0:T(8,128)(2,1)}, u32[]{:S(2)}) copy-start(bf16[256,1024]{1,0:T(8,128)(2,1)} %param.6) | copy-start | bytes 1572868
  6.5 78.2 %all-gather.3.cloned.1.call-start = ((), (), s32[]{:S(2)}) async-start(), calls=%async_computation.3 | async-start | bytes 6553600 | tf_op jit(solution)/shard_map/all_gather | solution.py:38
  46.7 241.0 %all-gather.5.cloned.1.call-start = ((), (), s32[]{:S(2)}) async-start(), calls=%async_computation.4 | async-start | bytes 6553600 | tf_op jit(solution)/shard_map/all_gather | solution.py:48
  230.5 20.3 %copy-start.2 = (f32[256,8]{0,1:T(8,128)S(1)}, f32[256,8]{0,1:T(8,128)}, u32[]{:S(2)}) copy-start(f32[256,8]{0,1:T(8,128)} %param.8) | copy-start | bytes 24580
  304.8 20.4 %copy-start.1 = (bf16[256,1024]{1,0:T(8,128)(2,1)S(1)}, bf16[256,1024]{1,0:T(8,128)(2,1)}, u32[]{:S(2)}) copy-start(bf16[256,1024]{1,0:T(8,128)(2,1)} %param.6) | copy-start | bytes 1572868
Sparse Core Ops, SparseCore 0:
  46.8 37.7 all-gather.2
  250.7 36.9 all-gather.4
where the time goes:
time: 333 us; the launch traced here: 332 us
  blocking collectives  103 us (31%)
  waiting for transfers between devices  74.5 us (22%)
  matrix products  73.8 us (22%)
  local copies, waits for them, and re-layouts  53.7 us (16%)
  between operations  13.6 us (4%)
  other arithmetic  13.2 us (4%)
    all_to_all x1, blocking collectives, device_body(): pieces = lax.all_to_all(part_out, 'tp', 1, 1, tiled=True)  62.8 us
    dot_general x1, matrix products, device_body(): jnp.einsum('erf,efd->erd', hidden, wd_loc, preferred_element_type=jnp.flo...  40.4 us
    all_gather x1, waiting for transfers between devices, device_body(): gathered = lax.all_gather(arrived, 'tp', axis=1, tiled=True)  37.7 us
    all_gather x1, waiting for transfers between devices, device_body(): lax.all_gather(returned, 'tp', axis=1, tiled=True)  36.7 us
    dot_general x1, matrix products, device_body(): jnp.einsum('erd,edf->erf', gathered, wu_loc, preferred_element_type=jnp.f...  33.4 us
    all_to_all x1, blocking collectives, device_body(): lax.all_to_all(outgoing, 'ep', 0, 2, tiled=True)  21.5 us
    all_to_all x1, blocking collectives, device_body(): lax.all_to_all(y_mine.reshape(local_experts, n_ep, slot_share, d_model),...  18.8 us
    gather x1, local copies, waits for them, and re-layouts, device_body(): picked = jnp.take(y_all, flat_slot, axis=0, mode='fill', fill_value=0)  14.2 us
  transfers between devices with their start and end apart: 2, of which 2 were waited for; matrix products, arithmetic and copies ran while one was open for 0% of the time, Pallas kernels for 0%

commit v1 on v0

v1 whole, which is shorter than its diff:
```python
import functools

import jax
import jax.numpy as jnp
from jax import lax
from jax.experimental import pallas as pl
from jax.experimental.pallas import tpu as pltpu
from jax.sharding import PartitionSpec as P

CAP_NUM = 5
CAP_DEN = 4
GROUP = 4
SLOTS = 5
LAG = 3
FAR = -100.0

F32 = jnp.float32
BF16 = jnp.bfloat16


def moe_kernel(cap, x_hbm, ids_hbm, gates_hbm, wg_hbm, wu_hbm, wd_hbm, out_hbm,
               wgu, wd, x_own, x_oth, ids_v, gates_v, tr, r_own, r_out, r_in, r_oth, g_own,
               pbuf, d2d, qbuf, qrx, qry, qrd, acc, outb,
               w_sem, in_sem, xs_sem, xr_sem, rs_sem, ds_sem, dr_sem, qs_sem, qr_sem, as_sem, ar_sem, o_sem):
    n_loc, d_model, ff = wg_hbm.shape
    n_groups = n_loc // GROUP
    tokens, n_top = ids_hbm.shape
    n_exp = 2 * n_loc
    pad = 24
    pair_rows = 2 * cap
    rows = GROUP * cap

    ep = lax.axis_index("ep")
    tp = lax.axis_index("tp")
    core = lax.rem(tp, 2)
    xx = tp // 2
    sib = {"tp": xx * 2 + 1 - core}
    xpeer = {"tp": (1 - xx) * 2 + core}
    ypeer = {"ep": 1 - ep}
    diag = {"ep": 1 - ep, "tp": (1 - xx) * 2 + core}

    def remote(src, dst, ssem, rsem, dev):
        return pltpu.make_async_remote_copy(src_ref=src, dst_ref=dst, send_sem=ssem, recv_sem=rsem,
                                            device_id=dev, device_id_type=pl.DeviceIdType.MESH)

    def weights(g, slot):
        first = g * GROUP
        return (
            pltpu.make_async_copy(wg_hbm.at[pl.ds(first, GROUP)], wgu.at[slot, :, :, 0:ff], w_sem.at[slot, 0]),
            pltpu.make_async_copy(wu_hbm.at[pl.ds(first, GROUP)], wgu.at[slot, :, :, ff:2 * ff], w_sem.at[slot, 1]),
            pltpu.make_async_copy(wd_hbm.at[pl.ds(first, GROUP)], wd.at[slot], w_sem.at[slot, 2]),
        )

    ids_cp = pltpu.make_async_copy(ids_hbm, ids_v, in_sem.at[0])
    gates_cp = pltpu.make_async_copy(gates_hbm, gates_v, in_sem.at[1])
    x_cp = pltpu.make_async_copy(x_hbm, x_own, in_sem.at[2])
    ids_cp.start()
    gates_cp.start()
    x_cp.start()
    for s in range(SLOTS):
        for cp in weights(s, s):
            cp.start()

    barrier = pltpu.get_barrier_semaphore()
    for dev in (sib, xpeer, ypeer, diag):
        pl.semaphore_signal(barrier, inc=1, device_id=dev, device_id_type=pl.DeviceIdType.MESH)
    pl.semaphore_wait(barrier, 4)

    x_cp.wait()
    x_send = remote(x_own.at[core], x_oth.at[core], xs_sem.at[0], xr_sem.at[0], ypeer)
    x_send.start()

    ids_cp.wait()
    gates_cp.wait()
    tr[...] = jnp.zeros_like(tr)
    tr[:, 0:n_top] = ids_v[...].astype(F32)
    ids_t = tr[...].T
    tr[:, 0:n_top] = gates_v[...]
    gates_t = tr[...].T
    exp_id = lax.broadcasted_iota(jnp.int32, (n_exp, tokens), 0).astype(F32)
    member = jnp.zeros((n_exp, tokens), F32)
    gate = jnp.zeros((n_exp, tokens), F32)
    for j in range(n_top):
        hit = exp_id == ids_t[j:j + 1, :]
        member = jnp.where(hit, 1.0, member)
        gate = jnp.where(hit, gates_t[j:j + 1, :], gate)
    before = (lax.broadcasted_iota(jnp.int32, (tokens, tokens), 0)
              < lax.broadcasted_iota(jnp.int32, (tokens, tokens), 1))
    before = jnp.where(before, 1.0, 0.0).astype(BF16)
    rank = jnp.dot(member.astype(BF16), before, preferred_element_type=F32)
    kept = jnp.logical_and(member > 0.5, rank < cap - 0.5)
    slot_no = jnp.where(kept, rank, FAR)
    r_own[...] = slot_no.reshape(2, n_loc, tokens)
    r_out[...] = slot_no.astype(BF16).reshape(2, n_loc, tokens)
    g1 = gate.astype(BF16).astype(F32)
    g2 = (gate - g1).astype(BF16).astype(F32)
    g3 = gate - g1 - g2
    g_own[0] = g1.reshape(2, n_loc, tokens)
    g_own[1] = g2.reshape(2, n_loc, tokens)
    g_own[2] = g3.reshape(2, n_loc, tokens)
    acc[...] = jnp.zeros_like(acc)

    r_send = remote(r_out.at[1 - ep], r_in, rs_sem.at[0], rs_sem.at[1], ypeer)
    r_send.start()
    r_send.wait()
    r_oth[...] = r_in[...].astype(F32)

    x_send.wait()
    x_fwd = remote(x_oth.at[core], x_oth.at[core], xs_sem.at[1], xr_sem.at[1], sib)
    x_fwd.start()
    x_fwd.wait()

    row24 = lax.broadcasted_iota(jnp.int32, (pad, tokens), 0).astype(F32)

    def mask24(r_row, odd):
        return (row24 - 4.0 if odd else row24) == r_row

    def d2d_copy(g, slot):
        return remote(pbuf.at[slot, pl.ds(2 * (1 - core), 2)], d2d.at[g], ds_sem.at[slot], dr_sem.at[g], sib)

    def q_copies(g):
        return (
            remote(qbuf.at[g, 1 - xx, 0], qrx.at[g], qs_sem.at[0, g], qr_sem.at[0, g], xpeer),
            remote(qbuf.at[g, xx, 1], qry.at[g], qs_sem.at[1, g], qr_sem.at[1, g], ypeer),
            remote(qbuf.at[g, 1 - xx, 1], qrd.at[g], qs_sem.at[2, g], qr_sem.at[2, g], diag),
        )

    def matmuls(g):
        slot = lax.rem(g, SLOTS)
        ps = lax.rem(g, 2)
        for cp in weights(g, slot):
            cp.wait()

        @pl.when(g >= 2)
        def _():
            d2d_copy(g - 2, ps).wait_send()

        def pick(r_ref, x_ref):
            sel = jnp.concatenate(
                [jnp.where(mask24(r_ref[pl.ds(g * GROUP + i, 1), :], i % 2), 1.0, 0.0) for i in range(GROUP)], axis=0)
            return jnp.dot(sel.astype(BF16), x_ref[...].reshape(tokens, d_model), preferred_element_type=F32)

        own = pick(r_own.at[ep], x_own)
        oth = pick(r_oth, x_oth)
        res = []
        for i in range(GROUP):
            lhs = jnp.concatenate([own[pad * i:pad * (i + 1)], oth[pad * i:pad * (i + 1)]], axis=0).astype(BF16)
            gu = jnp.dot(lhs, wgu[slot, i], preferred_element_type=F32)
            hid = (jax.nn.silu(gu[:, 0:ff]) * gu[:, ff:2 * ff]).astype(BF16)
            res.append(jnp.dot(hid, wd[slot, i], preferred_element_type=F32))
            if i % 2 == 1:
                r0, r1 = res[i - 1], res[i]
                for src in range(2):
                    base = src * rows + (i // 2) * pair_rows
                    o = src * pad
                    for b in range(4):
                        cols = slice(b * 256, (b + 1) * 256)
                        pbuf[ps, b, base:base + 16, :] = r0[o:o + 16, cols]
                        pbuf[ps, b, base + 16:base + 24, :] = r0[o + 16:o + 24, cols] + r1[o:o + 8, cols]
                        pbuf[ps, b, base + 24:base + 40, :] = r1[o + 8:o + 24, cols]
        d2d_copy(g, ps).start()

        @pl.when(g + SLOTS < n_groups)
        def _():
            for cp in weights(g + SLOTS, slot):
                cp.start()

    def chip_sum(g):
        ps = lax.rem(g, 2)
        d2d_copy(g, ps).wait_recv()
        for xi in range(2):
            q = (pbuf[ps, 2 * core + xi] + d2d[g, xi]).astype(BF16)
            qbuf[g, xi] = q.reshape(2, rows, 256)
        for cp in q_copies(g):
            cp.start()

    def combine(g):
        for cp in q_copies(g):
            cp.wait()
        y_own = (qbuf[g, xx, 0].astype(F32) + qrx[g].astype(F32)).astype(BF16)
        y_oth = (qry[g].astype(F32) + qrd[g].astype(F32)).astype(BF16)
        lhs, rhs = [], []
        for side, y in ((ep, y_own), (1 - ep, y_oth)):
            masks = [mask24(r_own[side, pl.ds(g * GROUP + i, 1), :], i % 2) for i in range(GROUP)]
            for k in range(3):
                c = [jnp.where(masks[i], g_own[k, side, pl.ds(g * GROUP + i, 1), :], 0.0) for i in range(GROUP)]
                for p in range(GROUP // 2):
                    c0, c1 = c[2 * p], c[2 * p + 1]
                    lhs += [c0[0:16], c0[16:24] + c1[0:8], c1[8:24]]
                rhs.append(y)
        lhs = jnp.concatenate(lhs, axis=0).astype(BF16)
        rhs = jnp.concatenate(rhs, axis=0)
        acc[...] += lax.dot_general(lhs, rhs, (((0,), (0,)), ((), ())), preferred_element_type=F32)

    def step(g, carry):
        @pl.when(g < n_groups)
        def _():
            matmuls(g)

        @pl.when(jnp.logical_and(g >= 1, g < n_groups + 1))
        def _():
            chip_sum(g - 1)

        @pl.when(g >= LAG)
        def _():
            combine(g - LAG)

        return carry

    lax.fori_loop(0, n_groups + LAG, step, 0)
    for g in (n_groups - 2, n_groups - 1):
        d2d_copy(g, g % 2).wait_send()

    mine = 2 * core + xx
    outb[mine] = acc[...].astype(BF16)
    to_sib = remote(outb.at[mine], outb.at[mine], as_sem.at[0], ar_sem.at[0], sib)
    to_x = remote(outb.at[mine], outb.at[mine], as_sem.at[1], ar_sem.at[1], xpeer)
    to_x.start()
    to_sib.start()
    to_x.wait()
    far = 2 * core + 1 - xx
    fwd = remote(outb.at[far], outb.at[far], as_sem.at[2], ar_sem.at[2], sib)
    fwd.start()
    to_sib.wait()
    fwd.wait()
    outs = [pltpu.make_async_copy(outb.at[b], out_hbm.at[:, pl.ds(b * 256, 256)], o_sem.at[b]) for b in range(4)]
    for cp in outs:
        cp.start()
    for cp in outs:
        cp.wait()


def solution(mesh):
    row_spec = P(("dp", "ep"), None)

    def device_body(x_loc, ids_loc, gates_loc, wg_loc, wu_loc, wd_loc):
        tokens, d_model = x_loc.shape
        n_top = ids_loc.shape[1]
        n_loc, _, ff = wg_loc.shape
        n_exp = 2 * n_loc
        cap = CAP_NUM * n_top * tokens // (CAP_DEN * n_exp)
        rows = GROUP * cap
        n_groups = n_loc // GROUP
        dma = pltpu.SemaphoreType.DMA
        anys = pl.BlockSpec(memory_space=pl.ANY)
        return pl.pallas_call(
            functools.partial(moe_kernel, cap),
            out_shape=jax.ShapeDtypeStruct((tokens, d_model), BF16),
            in_specs=[anys] * 6,
            out_specs=anys,
            scratch_shapes=[
                pltpu.VMEM((SLOTS, GROUP, d_model, 2 * ff), BF16),
                pltpu.VMEM((SLOTS, GROUP, ff, d_model), BF16),
                pltpu.VMEM((2, tokens // 2, d_model), BF16),
                pltpu.VMEM((2, tokens // 2, d_model), BF16),
                pltpu.VMEM((tokens, n_top), jnp.int32),
                pltpu.VMEM((tokens, n_top), F32),
                pltpu.VMEM((tokens, 128), F32),
                pltpu.VMEM((2, n_loc, tokens), F32),
                pltpu.VMEM((2, n_loc, tokens), BF16),
                pltpu.VMEM((n_loc, tokens), BF16),
                pltpu.VMEM((n_loc, tokens), F32),
                pltpu.VMEM((3, 2, n_loc, tokens), F32),
                pltpu.VMEM((2, 4, 2 * rows, 256), F32),
                pltpu.VMEM((n_groups, 2, 2 * rows, 256), F32),
                pltpu.VMEM((n_groups, 2, 2, rows, 256), BF16),
                pltpu.VMEM((n_groups, rows, 256), BF16),
                pltpu.VMEM((n_groups, rows, 256), BF16),
                pltpu.VMEM((n_groups, rows, 256), BF16),
                pltpu.VMEM((tokens, 256), F32),
                pltpu.VMEM((4, tokens, 256), BF16),
                dma((SLOTS, 3)), dma((3,)), dma((2,)), dma((2,)), dma((2,)), dma((2,)), dma((n_groups,)),
                dma((3, n_groups)), dma((3, n_groups)), dma((3,)), dma((3,)), dma((4,)),
            ],
            compiler_params=pltpu.CompilerParams(
                collective_id=0, has_side_effects=True, vmem_limit_bytes=67043328),
        )(x_loc.reshape(2, tokens // 2, d_model), ids_loc, gates_loc, wg_loc, wu_loc, wd_loc)

    return jax.shard_map(device_body, mesh=mesh,
                         in_specs=(row_spec, row_spec, row_spec, P("ep", None, "tp"), P("ep", None, "tp"), P("ep", "tp", None)),
                         out_specs=row_spec, check_vma=False)
```

time: 333 us -> 88.6 us (0.27)
  blocking collectives: 103 us -> 0 us
  Pallas kernels: 0 us -> 83.5 us
  waiting for transfers between devices: 74.5 us -> 0 us
  matrix products: 73.8 us -> 0 us
  local copies, waits for them, and re-layouts: 53.7 us -> 4.83 us
  between operations: 13.6 us -> 0.01 us
  other arithmetic: 13.2 us -> 0 us
    all_to_all x3 -> x0, blocking collectives: 103 us -> none  [the longest x1 62.8 us: device_body(): pieces = lax.all_to_all(part_out, 'tp', 1, 1, tiled=True)]
    pallas_call x0 -> x1, Pallas kernels: none -> 83.5 us  [device_body(): pl.pallas_call(functools.partial(moe_kernel, cap), out_shape=jax.ShapeDty...]
    all_gather x2 -> x0, waiting for transfers between devices: 74.5 us -> none  [the longest x1 37.7 us: device_body(): gathered = lax.all_gather(arrived, 'tp', axis=1, tiled=True)]
    dot_general x2 -> x0, matrix products: 73.8 us -> none  [the longest x1 40.4 us: device_body(): jnp.einsum('erf,efd->erd', hidden, wd_loc, preferred_element_type=jnp.flo...]
    gather x3 -> x0, local copies, waits for them, and re-layouts: 18.7 us -> none  [the longest x1 14.2 us: device_body(): picked = jnp.take(y_all, flat_slot, axis=0, mode='fill', fill_value=0)]
    reduce_sum x3 -> x0, other arithmetic: 10.7 us -> none  [the longest x1 6.19 us: device_body(): return jnp.sum(picked * gates_loc[:, :, None], axis=1).astype(jnp.bfloat16)]
    reshape x3 -> x0, local copies, waits for them, and re-layouts: 9.18 us -> none  [the longest x1 8.97 us: device_body(): lax.all_gather(returned, 'tp', axis=1, tiled=True)]
    all_gather x1 -> x0, local copies, waits for them, and re-layouts: 8.16 us -> none  [device_body(): lax.all_gather(returned, 'tp', axis=1, tiled=True)]
  transfers between devices with their start and end apart: 2 -> 0, of which waited for: 2 -> 0; matrix products, arithmetic and copies ran while one was open for 0% -> 0% of each run, Pallas kernels for 0% -> 0%
where the time goes in v1:
time: 88.6 us; the launch traced here: 88.3 us
  Pallas kernels  83.5 us (94%)
  local copies, waits for them, and re-layouts  4.83 us (5%)
    pallas_call x1, Pallas kernels, device_body(): pl.pallas_call(functools.partial(moe_kernel, cap), out_shape=jax.ShapeDty...  83.5 us
    unnamed x3, local copies, waits for them, and re-layouts  4.83 us

profile of v1, /device:TPU:0, one launch (start us, length us, event | category | flops | bytes accessed | tf_op | source)
XLA Modules:
  0.0 88.3 jit_solution(1964406580611363252)
XLA Ops:
  0.0 1.5 %copy.7.ids_hbm = s32[256,8]{1,0:T(8,128)} copy(s32[256,8]{0,1:T(8,128)} %param.7) | data formatting | bytes 16384 | tf_op args[1]
  1.5 1.5 %copy.8.gates_hbm = f32[256,8]{1,0:T(8,128)} copy(f32[256,8]{0,1:T(8,128)} %param.8) | data formatting | bytes 16384 | tf_op args[2]
  3.0 83.5 %shard_map.64 = bf16[256,1024]{1,0:T(8,128)(2,1)} custom-call(bf16[2,128,1024]{2,1,0:T(8,128)(2,1)} %bitcast.1, s32[256,8]{1,0:T(8,128)} %copy.7.ids_hbm, f32[256,8]{1,0:T(8,128)} %copy.8.gates_hbm, bf16[64,1024,384]{2,1,0:T(8,128)(2,1)} %wg_hbm.1, bf16[64,1024,384]{2,1,0:T(8,128)(2,1)} %wu_hbm.1, bf16[64,384,1024]{2,1,0:T(8,128)(2,1)} %wd_hbm.1), custom_call_target="tpu_custom_call" | custom-call | tf_op jit(solution)/shard_map/pallas_call | solution.py:246
  86.5 1.9 %copy.10 = bf16[256,1024]{1,0:T(8,128)(2,1)} copy(bf16[256,1024]{1,0:T(8,128)(2,1)} %shard_map.64) | data formatting | bytes 1048576

commit v2 on v1

--- a/solution.py
+++ b/solution.py
@@ -19,12 +19,12 @@
 
 
 def moe_kernel(cap, x_hbm, ids_hbm, gates_hbm, wg_hbm, wu_hbm, wd_hbm, out_hbm,
-               wgu, wd, x_own, x_oth, ids_v, gates_v, tr, r_own, r_out, r_in, r_oth, g_own,
+               wgu, wd, x_own, x_oth, ids_v, gates_v, r_own, r_out, r_in, r_oth, g_own, lhs_v,
                pbuf, d2d, qbuf, qrx, qry, qrd, acc, outb,
                w_sem, in_sem, xs_sem, xr_sem, rs_sem, ds_sem, dr_sem, qs_sem, qr_sem, as_sem, ar_sem, o_sem):
     n_loc, d_model, ff = wg_hbm.shape
     n_groups = n_loc // GROUP
-    tokens, n_top = ids_hbm.shape
+    n_top, tokens = ids_hbm.shape
     n_exp = 2 * n_loc
     pad = 24
     pair_rows = 2 * cap
@@ -59,7 +59,7 @@
     x_cp.start()
     for s in range(SLOTS):
         for cp in weights(s, s):
-            cp.start()
+            cp.start(priority=1)
 
     barrier = pltpu.get_barrier_semaphore()
     for dev in (sib, xpeer, ypeer, diag):
@@ -72,11 +72,8 @@
 
     ids_cp.wait()
     gates_cp.wait()
-    tr[...] = jnp.zeros_like(tr)
-    tr[:, 0:n_top] = ids_v[...].astype(F32)
-    ids_t = tr[...].T
-    tr[:, 0:n_top] = gates_v[...]
-    gates_t = tr[...].T
+    ids_t = ids_v[...].astype(F32)
+    gates_t = gates_v[...]
     exp_id = lax.broadcasted_iota(jnp.int32, (n_exp, tokens), 0).astype(F32)
     member = jnp.zeros((n_exp, tokens), F32)
     gate = jnp.zeros((n_exp, tokens), F32)
@@ -115,6 +112,15 @@
     def mask24(r_row, odd):
         return (row24 - 4.0 if odd else row24) == r_row
 
+    def pick(g):
+        both = []
+        for r_ref, x_ref in ((r_own.at[ep], x_own), (r_oth, x_oth)):
+            sel = jnp.concatenate(
+                [jnp.where(mask24(r_ref[pl.ds(g * GROUP + i, 1), :], i % 2), 1.0, 0.0) for i in range(GROUP)], axis=0)
+            both.append(jnp.dot(sel.astype(BF16), x_ref[...].reshape(tokens, d_model), preferred_element_type=F32))
+        parts = [v[pad * i:pad * (i + 1)] for i in range(GROUP) for v in both]
+        return jnp.concatenate(parts, axis=0).astype(BF16)
+
     def d2d_copy(g, slot):
         return remote(pbuf.at[slot, pl.ds(2 * (1 - core), 2)], d2d.at[g], ds_sem.at[slot], dr_sem.at[g], sib)
 
@@ -135,19 +141,21 @@
         def _():
             d2d_copy(g - 2, ps).wait_send()
 
-        def pick(r_ref, x_ref):
-            sel = jnp.concatenate(
-                [jnp.where(mask24(r_ref[pl.ds(g * GROUP + i, 1), :], i % 2), 1.0, 0.0) for i in range(GROUP)], axis=0)
-            return jnp.dot(sel.astype(BF16), x_ref[...].reshape(tokens, d_model), preferred_element_type=F32)
-
-        own = pick(r_own.at[ep], x_own)
-        oth = pick(r_oth, x_oth)
+        def up(i):
+            return jnp.dot(lhs_v[pad * 2 * i:pad * 2 * (i + 1), :], wgu[slot, i], preferred_element_type=F32)
+
+        def down(gu, i):
+            hid = (jax.nn.silu(gu[:, 0:ff]) * gu[:, ff:2 * ff]).astype(BF16)
+            return jnp.dot(hid, wd[slot, i], preferred_element_type=F32)
+
+        gu = [up(0)]
         res = []
         for i in range(GROUP):
-            lhs = jnp.concatenate([own[pad * i:pad * (i + 1)], oth[pad * i:pad * (i + 1)]], axis=0).astype(BF16)
-            gu = jnp.dot(lhs, wgu[slot, i], preferred_element_type=F32)
-            hid = (jax.nn.silu(gu[:, 0:ff]) * gu[:, ff:2 * ff]).astype(BF16)
-            res.append(jnp.dot(hid, wd[slot, i], preferred_element_type=F32))
+            if i + 1 < GROUP:
+                gu.append(up(i + 1))
+            else:
+                nxt = pick(jnp.minimum(g + 1, n_groups - 1))
+            res.append(down(gu[i], i))
             if i % 2 == 1:
                 r0, r1 = res[i - 1], res[i]
                 for src in range(2):
@@ -158,12 +166,13 @@
                         pbuf[ps, b, base:base + 16, :] = r0[o:o + 16, cols]
                         pbuf[ps, b, base + 16:base + 24, :] = r0[o + 16:o + 24, cols] + r1[o:o + 8, cols]
                         pbuf[ps, b, base + 24:base + 40, :] = r1[o + 8:o + 24, cols]
+        lhs_v[...] = nxt
         d2d_copy(g, ps).start()
 
         @pl.when(g + SLOTS < n_groups)
         def _():
             for cp in weights(g + SLOTS, slot):
-                cp.start()
+                cp.start(priority=1)
 
     def chip_sum(g):
         ps = lax.rem(g, 2)
@@ -191,6 +200,8 @@
         lhs = jnp.concatenate(lhs, axis=0).astype(BF16)
         rhs = jnp.concatenate(rhs, axis=0)
         acc[...] += lax.dot_general(lhs, rhs, (((0,), (0,)), ((), ())), preferred_element_type=F32)
+
+    lhs_v[...] = pick(0)
 
     def step(g, carry):
         @pl.when(g < n_groups)
@@ -253,14 +264,14 @@
                 pltpu.VMEM((SLOTS, GROUP, ff, d_model), BF16),
                 pltpu.VMEM((2, tokens // 2, d_model), BF16),
                 pltpu.VMEM((2, tokens // 2, d_model), BF16),
-                pltpu.VMEM((tokens, n_top), jnp.int32),
-                pltpu.VMEM((tokens, n_top), F32),
-                pltpu.VMEM((tokens, 128), F32),
+                pltpu.VMEM((n_top, tokens), jnp.int32),
+                pltpu.VMEM((n_top, tokens), F32),
                 pltpu.VMEM((2, n_loc, tokens), F32),
                 pltpu.VMEM((2, n_loc, tokens), BF16),
                 pltpu.VMEM((n_loc, tokens), BF16),
                 pltpu.VMEM((n_loc, tokens), F32),
                 pltpu.VMEM((3, 2, n_loc, tokens), F32),
+                pltpu.VMEM((GROUP * 48, d_model), BF16),
                 pltpu.VMEM((2, 4, 2 * rows, 256), F32),
                 pltpu.VMEM((n_groups, 2, 2 * rows, 256), F32),
                 pltpu.VMEM((n_groups, 2, 2, rows, 256), BF16),
@@ -274,7 +285,7 @@
             ],
             compiler_params=pltpu.CompilerParams(
                 collective_id=0, has_side_effects=True, vmem_limit_bytes=67043328),
-        )(x_loc.reshape(2, tokens // 2, d_model), ids_loc, gates_loc, wg_loc, wu_loc, wd_loc)
+        )(x_loc.reshape(2, tokens // 2, d_model), ids_loc.T, gates_loc.T, wg_loc, wu_loc, wd_loc)
 
     return jax.shard_map(device_body, mesh=mesh,
                          in_specs=(row_spec, row_spec, row_spec, P("ep", None, "tp"), P("ep", None, "tp"), P("ep", "tp", None)),

time: 88.6 us -> 64.9 us (0.73)
  Pallas kernels: 83.5 us -> 62.9 us
  local copies, waits for them, and re-layouts: 4.83 us -> 1.87 us
    pallas_call x1, Pallas kernels: 83.5 us -> 62.9 us  [device_body(): pl.pallas_call(functools.partial(moe_kernel, cap), out_shape=jax.ShapeDty...]
    unnamed x3 -> x1, local copies, waits for them, and re-layouts: 4.83 us -> 1.87 us
where the time goes in v2:
time: 64.9 us; the launch traced here: 64.8 us
  Pallas kernels  62.9 us (97%)
  local copies, waits for them, and re-layouts  1.87 us (3%)
    pallas_call x1, Pallas kernels, device_body(): pl.pallas_call(functools.partial(moe_kernel, cap), out_shape=jax.ShapeDty...  62.9 us
    unnamed x1, local copies, waits for them, and re-layouts  1.87 us

profile of v2, /device:TPU:0, one launch (start us, length us, event | category | flops | bytes accessed | tf_op | source)
XLA Modules:
  0.0 64.8 jit_solution(1957742361098643955)
XLA Ops:
  0.0 62.9 %shard_map.64 = bf16[256,1024]{1,0:T(8,128)(2,1)} custom-call(bf16[2,128,1024]{2,1,0:T(8,128)(2,1)} %bitcast.3, s32[8,256]{1,0:T(8,128)} %bitcast.4, f32[8,256]{1,0:T(8,128)} %bitcast.5, bf16[64,1024,384]{2,1,0:T(8,128)(2,1)} %wg_hbm.1, bf16[64,1024,384]{2,1,0:T(8,128)(2,1)} %wu_hbm.1, bf16[64,384,1024]{2,1,0:T(8,128)(2,1)} %wd_hbm.1), custom_call_target="tpu_custom_call" | custom-call | tf_op jit(solution)/shard_map/pallas_call | solution.py:257
  62.9 1.9 %copy.8 = bf16[256,1024]{1,0:T(8,128)(2,1)} copy(bf16[256,1024]{1,0:T(8,128)(2,1)} %shard_map.64) | data formatting | bytes 1048576

commit v3 on v2

v3 whole, which is shorter than its diff:
```python
import functools

import jax
import jax.numpy as jnp
from jax import lax
from jax.experimental import pallas as pl
from jax.experimental.pallas import tpu as pltpu
from jax.sharding import PartitionSpec as P

CAP_NUM = 5
CAP_DEN = 4
PAIRS = 2
SLOTS = 10
TAIL = 4
LAG = 4
FAR = -100.0

F32 = jnp.float32
BF16 = jnp.bfloat16


def moe_kernel(cap, x_hbm, ids_hbm, gates_hbm, wg_hbm, wu_hbm, wd_hbm, out_hbm,
               wgu, wd, x_own, x_oth, ids_v, gates_v, r_own, r_out, r_in, r_oth, g_own, lhs_v,
               pbuf, d2d, qbuf, qrx, qry, qrd, acc,
               w_sem, in_sem, xs_sem, xr_sem, rs_sem, ds_sem, dr_sem, qs_sem, qr_sem, as_sem, ar_sem):
    n_loc, d_model, ff = wg_hbm.shape
    n_pairs = n_loc // 2
    n_main = (n_pairs - TAIL) // PAIRS
    n_units = n_main + TAIL
    n_top, tokens = ids_hbm.shape
    n_exp = 2 * n_loc
    pad = 24
    pair_rows = 2 * cap

    ep = lax.axis_index("ep")
    tp = lax.axis_index("tp")
    core = lax.rem(tp, 2)
    xx = tp // 2
    sib = {"tp": xx * 2 + 1 - core}
    xpeer = {"tp": (1 - xx) * 2 + core}
    ypeer = {"ep": 1 - ep}
    diag = {"ep": 1 - ep, "tp": (1 - xx) * 2 + core}

    def remote(src, dst, ssem, rsem, dev):
        return pltpu.make_async_remote_copy(src_ref=src, dst_ref=dst, send_sem=ssem, recv_sem=rsem,
                                            device_id=dev, device_id_type=pl.DeviceIdType.MESH)

    def weights(p):
        slot = lax.rem(p, SLOTS)
        two = pl.ds(2 * p, 2)
        return (
            pltpu.make_async_copy(wg_hbm.at[two], wgu.at[slot, :, :, 0:ff], w_sem.at[slot, 0]),
            pltpu.make_async_copy(wu_hbm.at[two], wgu.at[slot, :, :, ff:2 * ff], w_sem.at[slot, 1]),
            pltpu.make_async_copy(wd_hbm.at[two], wd.at[slot], w_sem.at[slot, 2]),
        )

    def start_weights(p):
        for cp in weights(p):
            cp.start(priority=1)

    ids_cp = pltpu.make_async_copy(ids_hbm, ids_v, in_sem.at[0])
    gates_cp = pltpu.make_async_copy(gates_hbm, gates_v, in_sem.at[1])
    x_cp = pltpu.make_async_copy(x_hbm, x_own, in_sem.at[2])
    ids_cp.start()
    gates_cp.start()
    x_cp.start()
    for p in range(SLOTS):
        start_weights(p)

    barrier = pltpu.get_barrier_semaphore()
    for dev in (sib, xpeer, ypeer, diag):
        pl.semaphore_signal(barrier, inc=1, device_id=dev, device_id_type=pl.DeviceIdType.MESH)
    pl.semaphore_wait(barrier, 4)

    x_cp.wait()
    x_send = remote(x_own.at[core], x_oth.at[core], xs_sem.at[0], xr_sem.at[0], ypeer)
    x_send.start()

    ids_cp.wait()
    gates_cp.wait()
    ids_t = ids_v[...].astype(F32)
    gates_t = gates_v[...]
    exp_id = lax.broadcasted_iota(jnp.int32, (n_exp, tokens), 0).astype(F32)
    member = jnp.zeros((n_exp, tokens), F32)
    gate = jnp.zeros((n_exp, tokens), F32)
    for j in range(n_top):
        hit = exp_id == ids_t[j:j + 1, :]
        member = jnp.where(hit, 1.0, member)
        gate = jnp.where(hit, gates_t[j:j + 1, :], gate)
    before = (lax.broadcasted_iota(jnp.int32, (tokens, tokens), 0)
              < lax.broadcasted_iota(jnp.int32, (tokens, tokens), 1))
    before = jnp.where(before, 1.0, 0.0).astype(BF16)
    rank = jnp.dot(member.astype(BF16), before, preferred_element_type=F32)
    kept = jnp.logical_and(member > 0.5, rank < cap - 0.5)
    slot_no = jnp.where(kept, rank, FAR)
    r_own[...] = slot_no.reshape(2, n_loc, tokens)
    r_out[...] = slot_no.astype(BF16).reshape(2, n_loc, tokens)
    g1 = gate.astype(BF16).astype(F32)
    g2 = (gate - g1).astype(BF16).astype(F32)
    g3 = gate - g1 - g2
    g_own[0] = g1.reshape(2, n_loc, tokens)
    g_own[1] = g2.reshape(2, n_loc, tokens)
    g_own[2] = g3.reshape(2, n_loc, tokens)
    acc[...] = jnp.zeros_like(acc)

    r_send = remote(r_out.at[1 - ep], r_in, rs_sem.at[0], rs_sem.at[1], ypeer)
    r_send.start()
    r_send.wait()
    r_oth[...] = r_in[...].astype(F32)

    x_send.wait()
    x_fwd = remote(x_oth.at[core], x_oth.at[core], xs_sem.at[1], xr_sem.at[1], sib)
    x_fwd.start()
    x_fwd.wait()

    row24 = lax.broadcasted_iota(jnp.int32, (pad, tokens), 0).astype(F32)

    def mask24(r_row, odd):
        return (row24 - 4.0 if odd else row24) == r_row

    def pick(p0):
        both = []
        for r_ref, x_ref in ((r_own.at[ep], x_own), (r_oth, x_oth)):
            sel = jnp.concatenate(
                [jnp.where(mask24(r_ref[pl.ds(2 * p0 + i, 1), :], i % 2), 1.0, 0.0) for i in range(2 * PAIRS)], axis=0)
            both.append(jnp.dot(sel.astype(BF16), x_ref[...].reshape(tokens, d_model), preferred_element_type=F32))
        parts = [v[pad * i:pad * (i + 1)] for i in range(2 * PAIRS) for v in both]
        return jnp.concatenate(parts, axis=0).astype(BF16)

    def d2d_copy(unit):
        u, p0, n = unit
        slot = lax.rem(u, 2)
        return remote(pbuf.at[slot, pl.ds(0, n), pl.ds(2 * (1 - core), 2)], d2d.at[pl.ds(p0, n)],
                      ds_sem.at[slot], dr_sem.at[u], sib)

    def q_copies(unit):
        u, p0, n = unit
        ps = pl.ds(p0, n)
        return (
            remote(qbuf.at[1 - xx, 0, ps], qrx.at[ps], qs_sem.at[0, u], qr_sem.at[0, u], xpeer),
            remote(qbuf.at[xx, 1, ps], qry.at[ps], qs_sem.at[1, u], qr_sem.at[1, u], ypeer),
            remote(qbuf.at[1 - xx, 1, ps], qrd.at[ps], qs_sem.at[2, u], qr_sem.at[2, u], diag),
        )

    def matmuls(unit, lhs0, nxt_pair, split):
        u, p0, n = unit
        ps = lax.rem(u, 2)
        cps = [weights(p0 + i) for i in range(n)]
        for cp in cps:
            cp[0].wait()
            cp[1].wait()
        if not split:
            for cp in cps:
                cp[2].wait()
        slots = [lax.rem(p0 + i, SLOTS) for i in range(n)]

        def up(i):
            lhs = lhs_v[lhs0 + 2 * pad * i:lhs0 + 2 * pad * (i + 1), :]
            return jnp.dot(lhs, wgu[slots[i // 2], i % 2], preferred_element_type=F32)

        def act(gu):
            return (jax.nn.silu(gu[:, 0:ff]) * gu[:, ff:2 * ff]).astype(BF16)

        def down(hid, i):
            return jnp.dot(hid, wd[slots[i // 2], i % 2], preferred_element_type=F32)

        def put(i, r0, r1):
            for src in range(2):
                base = src * pair_rows
                o = src * pad
                for b in range(4):
                    cols = slice(b * 256, (b + 1) * 256)
                    pbuf[ps, i, b, base:base + 16, :] = r0[o:o + 16, cols]
                    pbuf[ps, i, b, base + 16:base + 24, :] = r0[o + 16:o + 24, cols] + r1[o:o + 8, cols]
                    pbuf[ps, i, b, base + 24:base + 40, :] = r1[o + 8:o + 24, cols]

        nxt = None
        if split:
            hids = [act(g) for g in [up(i) for i in range(2 * n)]]
            for cp in cps:
                cp[2].wait()
            res = [down(h, i) for i, h in enumerate(hids)]
            for i in range(n):
                put(i, res[2 * i], res[2 * i + 1])
        else:
            gu = [up(0)]
            res = []
            for i in range(2 * n):
                if i + 1 < 2 * n:
                    gu.append(up(i + 1))
                elif nxt_pair is not None:
                    nxt = pick(nxt_pair)
                res.append(down(act(gu[i]), i))
                if i % 2 == 1:
                    put(i // 2, res[i - 1], res[i])
        if nxt is not None:
            lhs_v[...] = nxt
        d2d_copy(unit).start()

    def chip_sum(unit):
        u, p0, n = unit
        ps = lax.rem(u, 2)
        d2d_copy(unit).wait_recv()
        for i in range(n):
            for xi in range(2):
                q = (pbuf[ps, i, 2 * core + xi] + d2d[p0 + i, xi]).astype(BF16)
                qbuf[xi, 0, p0 + i] = q[0:pair_rows]
                qbuf[xi, 1, p0 + i] = q[pair_rows:2 * pair_rows]
        for cp in q_copies(unit):
            cp.start()

    def combine(unit):
        u, p0, n = unit
        for cp in q_copies(unit):
            cp.wait()
        lhs, rhs = [], []
        for here in (True, False):
            side = ep if here else 1 - ep
            y = []
            for i in range(n):
                if here:
                    parts = qbuf[xx, 0, p0 + i], qrx[p0 + i]
                else:
                    parts = qry[p0 + i], qrd[p0 + i]
                y.append(parts[0].astype(F32) + parts[1].astype(F32))
            for k in range(3):
                for i in range(n):
                    c = []
                    for odd in range(2):
                        e = pl.ds(2 * (p0 + i) + odd, 1)
                        c.append(jnp.where(mask24(r_own[side, e, :], odd), g_own[k, side, e, :], 0.0))
                    lhs += [c[0][0:16], c[0][16:24] + c[1][0:8], c[1][8:24]]
                    rhs.append(y[i])
        lhs = jnp.concatenate(lhs, axis=0).astype(BF16)
        rhs = jnp.concatenate(rhs, axis=0).astype(BF16)
        acc[...] += lax.dot_general(lhs, rhs, (((0,), (0,)), ((), ())), preferred_element_type=F32)

    def main_unit(u):
        return u, PAIRS * u, PAIRS

    lhs_v[...] = pick(0)

    def step(u, carry):
        @pl.when(u >= 2)
        def _():
            d2d_copy(main_unit(u - 2)).wait_send()

        matmuls(main_unit(u), 0, PAIRS * (u + 1), False)
        for i in range(PAIRS):
            p = PAIRS * u + i + SLOTS

            @pl.when(p < n_pairs)
            def _():
                start_weights(p)

        @pl.when(u >= 1)
        def _():
            chip_sum(main_unit(u - 1))

        @pl.when(u >= LAG)
        def _():
            combine(main_unit(u - LAG))

        return carry

    lax.fori_loop(0, n_main, step, 0)

    units = [main_unit(u) for u in range(n_main)]
    units += [(n_main + t, n_main * PAIRS + t, 1) for t in range(TAIL)]
    for t in range(TAIL):
        u = n_main + t
        last = t == TAIL - 1
        d2d_copy(units[u - 2]).wait_send()
        nxt_pair = units[u][1] + 1 if t % 2 == 1 and not last else None
        matmuls(units[u], 2 * 2 * pad * (t % 2), nxt_pair, False)
        chip_sum(units[u - 1])
    chip_sum(units[n_units - 1])
    for u in range(n_main - LAG, n_units):
        combine(units[u])
    for u in range(n_units - 2, n_units):
        d2d_copy(units[u]).wait_send()

    mine = 2 * core + xx

    def blk(b):
        return out_hbm.at[:, pl.ds(pl.multiple_of(b * 256, 256), 256)]

    out_hbm[:, pl.ds(pl.multiple_of(mine * 256, 256), 256)] = acc[...].astype(BF16)
    to_sib = remote(blk(mine), blk(mine), as_sem.at[0], ar_sem.at[0], sib)
    to_x = remote(blk(mine), blk(mine), as_sem.at[1], ar_sem.at[1], xpeer)
    to_x.start()
    to_sib.start()
    to_x.wait()
    far = 2 * core + 1 - xx
    fwd = remote(blk(far), blk(far), as_sem.at[2], ar_sem.at[2], sib)
    fwd.start()
    to_sib.wait()
    fwd.wait()


def solution(mesh):
    row_spec = P(("dp", "ep"), None)

    def device_body(x_loc, ids_loc, gates_loc, wg_loc, wu_loc, wd_loc):
        tokens, d_model = x_loc.shape
        n_top = ids_loc.shape[1]
        n_loc, _, ff = wg_loc.shape
        n_exp = 2 * n_loc
        cap = CAP_NUM * n_top * tokens // (CAP_DEN * n_exp)
        rows = 2 * cap
        n_pairs = n_loc // 2
        n_units = (n_pairs - TAIL) // PAIRS + TAIL
        dma = pltpu.SemaphoreType.DMA
        anys = pl.BlockSpec(memory_space=pl.ANY)
        return pl.pallas_call(
            functools.partial(moe_kernel, cap),
            out_shape=pltpu.VMEM((tokens, d_model), BF16),
            in_specs=[anys] * 6,
            out_specs=pl.BlockSpec(memory_space=pltpu.VMEM),
            scratch_shapes=[
                pltpu.VMEM((SLOTS, 2, d_model, 2 * ff), BF16),
                pltpu.VMEM((SLOTS, 2, ff, d_model), BF16),
                pltpu.VMEM((2, tokens // 2, d_model), BF16),
                pltpu.VMEM((2, tokens // 2, d_model), BF16),
                pltpu.VMEM((n_top, tokens), jnp.int32),
                pltpu.VMEM((n_top, tokens), F32),
                pltpu.VMEM((2, n_loc, tokens), F32),
                pltpu.VMEM((2, n_loc, tokens), BF16),
                pltpu.VMEM((n_loc, tokens), BF16),
                pltpu.VMEM((n_loc, tokens), F32),
                pltpu.VMEM((3, 2, n_loc, tokens), F32),
                pltpu.VMEM((PAIRS * 2 * 48, d_model), BF16),
                pltpu.VMEM((2, PAIRS, 4, 2 * rows, 256), F32),
                pltpu.VMEM((n_pairs, 2, 2 * rows, 256), F32),
                pltpu.VMEM((2, 2, n_pairs, rows, 256), BF16),
                pltpu.VMEM((n_pairs, rows, 256), BF16),
                pltpu.VMEM((n_pairs, rows, 256), BF16),
                pltpu.VMEM((n_pairs, rows, 256), BF16),
                pltpu.VMEM((tokens, 256), F32),
                dma((SLOTS, 3)), dma((3,)), dma((2,)), dma((2,)), dma((2,)), dma((2,)), dma((n_units,)),
                dma((3, n_units)), dma((3, n_units)), dma((3,)), dma((3,)),
            ],
            compiler_params=pltpu.CompilerParams(
                collective_id=0, has_side_effects=True, vmem_limit_bytes=63 * 1024 * 1024),
        )(x_loc.reshape(2, tokens // 2, d_model), ids_loc.T, gates_loc.T, wg_loc, wu_loc, wd_loc)

    return jax.shard_map(device_body, mesh=mesh,
                         in_specs=(row_spec, row_spec, row_spec, P("ep", None, "tp"), P("ep", None, "tp"), P("ep", "tp", None)),
                         out_specs=row_spec, check_vma=False)
```

time: 64.9 us -> 60.7 us (0.935)
  Pallas kernels: 62.9 us -> 59.8 us
  local copies, waits for them, and re-layouts: 1.87 us -> 0.8 us
    pallas_call x1, Pallas kernels: 62.9 us -> 59.8 us  [device_body(): pl.pallas_call(functools.partial(moe_kernel, cap), out_shape=pltpu.VMEM((...]
    unnamed x1, local copies, waits for them, and re-layouts: 1.87 us -> 0.8 us
where the time goes in v3:
time: 60.7 us; the launch traced here: 60.6 us
  Pallas kernels  59.8 us (99%)
  local copies, waits for them, and re-layouts  0.8 us (1%)
    pallas_call x1, Pallas kernels, device_body(): pl.pallas_call(functools.partial(moe_kernel, cap), out_shape=pltpu.VMEM((...  59.8 us

profile of v3, /device:TPU:0, one launch (start us, length us, event | category | flops | bytes accessed | tf_op | source)
XLA Modules:
  0.0 60.6 jit_solution(76636590845238420)
XLA Ops:
  0.0 59.8 %shard_map.64 = bf16[256,1024]{1,0:T(8,128)(2,1)S(1)} custom-call(bf16[2,128,1024]{2,1,0:T(8,128)(2,1)} %bitcast.3, s32[8,256]{1,0:T(8,128)} %bitcast.4, f32[8,256]{1,0:T(8,128)} %bitcast.5, bf16[64,1024,384]{2,1,0:T(8,128)(2,1)} %wg_hbm.1, bf16[64,1024,384]{2,1,0:T(8,128)(2,1)} %wu_hbm.1, bf16[64,384,1024]{2,1,0:T(8,128)(2,1)} %wd_hbm.1), custom_call_target="tpu_custom_call" | custom-call | tf_op jit(solution)/shard_map/pallas_call | solution.py:315
  59.8 0.8 %copy.8 = bf16[256,1024]{1,0:T(8,128)(2,1)} copy(bf16[256,1024]{1,0:T(8,128)(2,1)S(1)} %shard_map.64) | data formatting | bytes 1048576
